TPU v7x, 32 devices: a whole 2x2x4 slice. The times are simulated.
32 devices in a mesh: rep: 2 (over x), shard: 16 (over z, y, core).
Axes of the slice: x: 2, y: 2, z: 4, core: 2. Of those that a mesh axis runs over, the one named last changes fastest.
Arguments:
- tokens_x: bfloat16 [8192, 4096], P(('rep', 'shard')), may hold values from -6 to 6
- key_grad: bfloat16 [8192, 1024], P(('rep', 'shard')), may hold values from -0.06591797 to 0.06591797
- left_root: bfloat16 [64, 512, 512], P('shard'), may hold values from -1 to 3
- slot_grads: bfloat16 [64, 512, 512], P('shard'), may hold values from -6 to 6
- right_root: bfloat16 [64, 512, 512], P('shard'), may hold values from -1 to 3
- block_slot: int32 [32], replicated, may hold values from 0 to 63, as said below
Outputs:
- grad_key: float32 [4096, 1024], P('shard')
- update: bfloat16 [512, 32, 512], P('shard')
Inputs may be any that keep to these rules, and one draw needn't show every extreme that they name: `block_slot`: the entries are distinct; slot v is slot v % 4 of shard index v // 4; no shard index holds more than 4 blocks, and some shard index holds exactly 4.
All inputs are finite; a program needn't handle non-finite values.
Results may differ from a plain program's by a relative error of at most 0.006.
Values may be sent and summed in bfloat16 or wider, within the bound.
A program may use at most 128 MiB of HBM per device.

v0:
```python
import jax
import jax.numpy as jnp
from jax import lax
from jax.sharding import PartitionSpec as P


def column_term(features, cotangent):
    return lax.dot_general(
        features, cotangent, (((0,), (0,)), ((), ())), preferred_element_type=jnp.float32
    )


def precondition(left_block, grad_block, right_block):
    left_part = jnp.einsum(
        "sij,sjk->sik", left_block, grad_block, preferred_element_type=jnp.float32
    ).astype(jnp.bfloat16)
    return jnp.einsum(
        "sij,sjk->isk", left_part, right_block, preferred_element_type=jnp.float32
    ).astype(jnp.bfloat16)


def shards(tokens_x, key_grad, left_root, slot_grads, right_root, block_slot):
    n_shard = lax.axis_size("shard")
    n_rep = lax.axis_size("rep")
    own_rows = lax.psum_scatter(
        column_term(tokens_x, key_grad), "shard", scatter_dimension=0, tiled=True
    )
    grad_key = lax.psum(own_rows, "rep")
    slot_count = left_root.shape[0]
    half_slots = slot_count // n_rep
    first_slot = lax.axis_index("rep") * half_slots

    def own_half(values):
        return lax.dynamic_slice_in_dim(values, first_slot, half_slots, 0)

    product = precondition(own_half(left_root), own_half(slot_grads), own_half(right_root))
    received = lax.all_to_all(product, "shard", split_axis=0, concat_axis=1, tiled=True)
    joined = lax.all_gather(received, "rep", axis=1, tiled=True)
    owner = block_slot // slot_count
    within = block_slot % slot_count
    position = (
        within // half_slots * (n_shard * half_slots) + owner * half_slots + within % half_slots
    )
    update = jnp.take(joined, position, axis=1)
    return (grad_key, update)


def solution(mesh):
    return jax.shard_map(
        shards,
        mesh=mesh,
        in_specs=(
            P(("rep", "shard"), None),
            P(("rep", "shard"), None),
            P("shard", None, None),
            P("shard", None, None),
            P("shard", None, None),
            P(),
        ),
        out_specs=(P("shard", None), P("shard", None, None)),
        check_vma=False,
    )
```

profile of v0, /device:TPU:0, one launch (start us, length us, event | category | flops | bytes accessed | tf_op | source)
XLA Modules:
  0.0 247.9 jit_solution(18152596970215478150)
XLA Ops:
  8.0 0.0 copy-start
  8.0 0.0 reduce-scatter.2.cloned.1.call-start
  8.1 1.5 copy-done
  9.6 9.2 %fusion.9 = f32[4096,1024]{1,0:T(8,128)} fusion(bf16[256,4096]{1,0:T(8,128)(2,1)S(1)} %copy-done, bf16[256,1024]{1,0:T(8,128)(2,1)} %param.7), kind=kOutput, calls=%fused_computation.23 | convolution fusion | flops 2147483648 | bytes 19398656 | tf_op jit(solution)/shard_map/dot_general | solution.py:8
  18.8 0.0 reduce-scatter.2.cloned.1.call-update
  18.8 0.0 all-gather.2.cloned.1.call-start
  18.8 4.1 %fusion = bf16[512,2,512]{0,2,1:T(8,128)(2,1)} fusion(bf16[4,512,512]{2,1,0:T(8,128)(2,1)} %param.9, s32[]{:T(128)S(6)} %select_n.37, bf16[4,512,512]{2,1,0:T(8,128)(2,1)} %param.8, bf16[4,512,512]{2,1,0:T(8,128)(2,1)} %param.10), kind=kOutput, calls=%fused_computation.3 | convolution fusion | flops 1074790400 | bytes 4195840 | tf_op jit(solution)/shard_map/sij,sjk->isk/dot_general | solution.py:17
  22.9 2.5 %copy.14 = bf16[512,2,512]{2,1,0:T(2,128)(2,1)S(1)} copy(bf16[512,2,512]{0,2,1:T(8,128)(2,1)} %fusion) | data formatting | bytes 2097152 | tf_op jit(solution)/shard_map/convert_element_type | solution.py:19
  25.4 31.9 %all_to_all.18 = bf16[512,2,512]{2,1,0:T(2,128)(2,1)S(1)} all-to-all(bf16[512,2,512]{2,1,0:T(2,128)(2,1)S(1)} %copy.14), channel_id=1, replica_groups=mesh['rep'=2,'shard'=16] {'shard'}, dimensions={0} | all-to-all | bytes 2097152 | tf_op jit(solution)/shard_map/all_to_all | solution.py:37
  57.3 0.2 copy.15
  57.5 0.0 copy-start.1
  57.5 1.0 copy.16
  58.6 0.0 all-gather.2.cloned.1.call-update
  58.6 0.0 all-reduce.2.cloned.1.call-start
  58.6 140.4 %reduce-scatter.2.cloned.1.call-done = f32[256,1024]{1,0:T(8,128)} async-done(((f32[4096,1024]{1,0:T(8,128)}), f32[256,1024]{1,0:T(8,128)}) %reduce-scatter.2.cloned.1.call-update) | async-done | bytes 1048592 | tf_op jit(solution)/shard_map/reduce_scatter | solution.py:25
  199.0 0.0 all-reduce.2.cloned.1.call-update
  199.0 0.0 copy-done.1
  199.1 0.0 all-gather.2.cloned.1.call-done
  199.1 2.2 gather_fusion
  201.3 0.2 select_bitcast_fusion
  201.5 1.5 copy.17
  203.0 35.1 %all-reduce.2.cloned.1.call-done = f32[256,1024]{1,0:T(8,128)} async-done(((f32[256,1024]{1,0:T(8,128)}), f32[256,1024]{1,0:T(8,128)}) %all-reduce.2.cloned.1.call-update) | async-done | bytes 1048592 | tf_op jit(solution)/shard_map/psum | solution.py:28
  238.2 2.3 copy.20
  (2 shorter events, 0.0 us)
Async XLA Ops:
  8.0 1.6 copy-start
  8.0 191.0 %reduce-scatter.2.cloned.1.call-start = ((), (), s32[]{:S(2)}) async-start(), calls=%async_computation.2 | async-start | bytes 17825792 | tf_op jit(solution)/shard_map/reduce_scatter | solution.py:25
  18.8 180.3 %all-gather.2.cloned.1.call-start = ((), (), s32[]{:S(2)}) async-start(), calls=%async_computation.4 | async-start | bytes 3145728 | tf_op jit(solution)/shard_map/all_gather | solution.py:38
  57.5 141.5 %copy-start.1 = (s32[32]{0:T(128)S(1)}, s32[32]{0:T(128)}, u32[]{:S(2)}) copy-start(s32[32]{0:T(128)} %param.11) | copy-start | bytes 388
  58.6 179.6 %all-reduce.2.cloned.1.call-start = ((), (), s32[]{:S(2)}) async-start(), calls=%async_computation.3 | async-start | bytes 2097152 | tf_op jit(solution)/shard_map/psum | solution.py:28
Sparse Core Ops, SparseCore 0:
  18.9 180.0 reduce-scatter.1
Sparse Core Ops, SparseCore 1:
  58.7 33.3 all-gather.1
  199.1 39.0 all-reduce.1
where the time goes:
time: 248 us
  waiting for transfers between devices  176 us (71%)
  blocking collectives  31.9 us (13%)
  between operations  15.6 us (6%)
  matrix products  13.3 us (5%)
  local copies, waits for them, and re-layouts  11.3 us (5%)
    reduce_scatter x1, waiting for transfers between devices, shards(): lax.psum_scatter(column_term(tokens_x, key_grad), 'shard', scatter_dimens...  140 us
    psum x1, waiting for transfers between devices, shards(): grad_key = lax.psum(own_rows, 'rep')  35.1 us
    all_to_all x1, blocking collectives, shards(): lax.all_to_all(product, 'shard', split_axis=0, concat_axis=1, tiled=True)  31.9 us
    dot_general x1, matrix products, column_term(): lax.dot_general(features, cotangent, (((0,), (0,)), ((), ())), preferred_...  9.16 us
    unnamed x6, local copies, waits for them, and re-layouts  5.4 us
  transfers between devices with their start and end apart: 3, of which 2 were waited for; matrix products, arithmetic and copies ran while one was open for 5% of the time, Pallas kernels for 0%

commit v1 on v0

--- a/solution.py
+++ b/solution.py
@@ -34,7 +34,12 @@
         return lax.dynamic_slice_in_dim(values, first_slot, half_slots, 0)
 
     product = precondition(own_half(left_root), own_half(slot_grads), own_half(right_root))
-    received = lax.all_to_all(product, "shard", split_axis=0, concat_axis=1, tiled=True)
+    received = jnp.concatenate(
+        lax.all_to_all(
+            jnp.stack(jnp.split(product, lax.axis_size("shard"), axis=0)), "shard", 0, 0
+        ),
+        axis=1,
+    )
     joined = lax.all_gather(received, "rep", axis=1, tiled=True)
     owner = block_slot // slot_count
     within = block_slot % slot_count

time: 248 us -> 248 us (level)
  waiting for transfers between devices: 176 us -> 180 us
  local copies, waits for them, and re-layouts: 11.3 us -> 7.72 us
    reduce_scatter x1, waiting for transfers between devices: 140 us -> 145 us  [shards(): lax.psum_scatter(column_term(tokens_x, key_grad), 'shard', scatter_dimens...]
    convert_element_type x1 -> x0, local copies, waits for them, and re-layouts: 2.5 us -> none  [precondition(): return jnp.einsum('sij,sjk->isk', left_part, right_block, preferred_eleme...]
    unnamed x6 -> x21, local copies, waits for them, and re-layouts: 5.4 us -> 5.51 us
  transfers between devices with their start and end apart: 3 -> 3, of which waited for: 2 -> 2; matrix products, arithmetic and copies ran while one was open for 5% -> 3% of each run, Pallas kernels for 0% -> 0%
where the time goes in v1:
time: 248 us
  waiting for transfers between devices  180 us (73%)
  blocking collectives  32 us (13%)
  between operations  15.7 us (6%)
  matrix products  12.3 us (5%)
  local copies, waits for them, and re-layouts  7.72 us (3%)
    reduce_scatter x1, waiting for transfers between devices, shards(): lax.psum_scatter(column_term(tokens_x, key_grad), 'shard', scatter_dimens...  145 us
    psum x1, waiting for transfers between devices, shards(): grad_key = lax.psum(own_rows, 'rep')  35.1 us
    all_to_all x1, blocking collectives, shards(): lax.all_to_all(jnp.stack(jnp.split(product, lax.axis_size('shard'), axis=...  32 us
    dot_general x1, matrix products, column_term(): lax.dot_general(features, cotangent, (((0,), (0,)), ((), ())), preferred_...  9.16 us
    unnamed x21, local copies, waits for them, and re-layouts  5.51 us
  transfers between devices with their start and end apart: 3, of which 2 were waited for; matrix products, arithmetic and copies ran while one was open for 3% of the time, Pallas kernels for 0%

profile of v1, /device:TPU:0, one launch (start us, length us, event | category | flops | bytes accessed | tf_op | source)
XLA Modules:
  0.0 247.9 jit_solution(13406744691568452154)
XLA Ops:
  8.0 0.0 copy-start
  8.0 0.0 reduce-scatter.2.cloned.1.call-start
  8.1 1.5 copy-done
  9.6 9.2 %fusion.25 = f32[4096,1024]{1,0:T(8,128)} fusion(bf16[256,4096]{1,0:T(8,128)(2,1)S(1)} %copy-done, bf16[256,1024]{1,0:T(8,128)(2,1)} %param.7), kind=kOutput, calls=%fused_computation.55 | convolution fusion | flops 2147483648 | bytes 19398656 | tf_op jit(solution)/shard_map/dot_general | solution.py:8
  18.8 0.0 reduce-scatter.2.cloned.1.call-update
  18.8 0.0 all-gather.2.cloned.1.call-start
  18.8 3.1 %fusion = bf16[512,2,512]{2,0,1:T(8,128)(2,1)S(1)} fusion(bf16[4,512,512]{2,1,0:T(8,128)(2,1)} %param.9, s32[]{:T(128)S(6)} %select_n.37, bf16[4,512,512]{2,1,0:T(8,128)(2,1)} %param.8, bf16[4,512,512]{2,1,0:T(8,128)(2,1)} %param.10), kind=kOutput, calls=%fused_computation.3 | convolution fusion | flops 1074790400 | bytes 4195840 | tf_op jit(solution)/shard_map/sij,sjk->isk/dot_general | solution.py:17
  22.2 0.0 copy-start.1
  22.2 32.0 %all_to_all.5 = bf16[16,32,2,512]{3,1,2,0:T(8,128)(2,1)} all-to-all(bf16[16,32,2,512]{3,1,2,0:T(8,128)(2,1)S(1)} %fusion.6), channel_id=1, replica_groups=mesh['rep'=2,'shard'=16] {'shard'}, dimensions={0} | all-to-all | bytes 2097152 | tf_op jit(solution)/shard_map/all_to_all | solution.py:38
  54.2 0.0 all-gather.2.cloned.1.call-update
  54.2 0.0 all-reduce.2.cloned.1.call-start
  54.3 144.7 %reduce-scatter.2.cloned.1.call-done = f32[256,1024]{1,0:T(8,128)} async-done(((f32[4096,1024]{1,0:T(8,128)}), f32[256,1024]{1,0:T(8,128)}) %reduce-scatter.2.cloned.1.call-update) | async-done | bytes 1048592 | tf_op jit(solution)/shard_map/reduce_scatter | solution.py:25
  199.0 0.0 all-reduce.2.cloned.1.call-update
  199.0 0.0 copy-done.1
  199.1 0.0 all-gather.2.cloned.1.call-done
  199.1 2.2 gather_fusion
  201.3 0.2 select_bitcast_fusion
  201.5 1.5 copy.9
  203.0 35.1 %all-reduce.2.cloned.1.call-done = f32[256,1024]{1,0:T(8,128)} async-done(((f32[256,1024]{1,0:T(8,128)}), f32[256,1024]{1,0:T(8,128)}) %all-reduce.2.cloned.1.call-update) | async-done | bytes 1048592 | tf_op jit(solution)/shard_map/psum | solution.py:28
  238.2 2.3 copy.26
  (18 shorter events, 0.1 us)
Async XLA Ops:
  8.0 1.6 copy-start
  8.0 191.0 %reduce-scatter.2.cloned.1.call-start = ((), (), s32[]{:S(2)}) async-start(), calls=%async_computation.2 | async-start | bytes 17825792 | tf_op jit(solution)/shard_map/reduce_scatter | solution.py:25
  18.8 180.3 %all-gather.2.cloned.1.call-start = ((), (), s32[]{:S(2)}) async-start(), calls=%async_computation.4 | async-start | bytes 3145728 | tf_op jit(solution)/shard_map/all_gather | solution.py:43
  22.2 176.8 %copy-start.1 = (s32[32]{0:T(128)S(1)}, s32[32]{0:T(128)}, u32[]{:S(2)}) copy-start(s32[32]{0:T(128)} %param.11) | copy-start | bytes 388
  54.2 183.9 %all-reduce.2.cloned.1.call-start = ((), (), s32[]{:S(2)}) async-start(), calls=%async_computation.3 | async-start | bytes 2097152 | tf_op jit(solution)/shard_map/psum | solution.py:28
Sparse Core Ops, SparseCore 0:
  18.9 180.0 reduce-scatter.1
Sparse Core Ops, SparseCore 1:
  54.3 33.3 all-gather.1
  199.1 39.0 all-reduce.1
